TPU v7x, 32 devices: a whole 2x2x4 slice. The times are simulated.
32 devices in a mesh: parts: 2 (over y), section: 2 (over core), tp: 8 (over z, x).
Axes of the slice: x: 2, y: 2, z: 4, core: 2. Of those that a mesh axis runs over, the one named last changes fastest.
Arguments:
- prompt_rows: bfloat16 [128, 8192], P(('parts', 'section', 'tp')), parts along dimension 0, may hold values from -72 to 72
- query_weight: bfloat16 [8192, 8192], P(None, 'tp'), may hold values from -0.0625 to 0.0625
- cache_weight: bfloat16 [8, 8192, 256], P('tp'), may hold values from -1 to 1, as said below
- output_weight: bfloat16 [8192, 8192], P('tp'), may hold values from -0.0625 to 0.0625
- documents: int32 [128], P('parts'), parts along dimension 0, may hold values from 0 to 3, never falling along the last dimension, each value on 1 to 32 neighbouring positions
- page_table: int32 [24], P('parts'), parts along dimension 0, may hold values from 0 to 15, as said below
Outputs:
- branch_output: bfloat16 [128, 8192], P(('parts', 'section', 'tp')), parts along dimension 0
- page_pool: bfloat16 [32, 8, 2048], P(('parts', 'section', 'tp')), parts along dimension 0
There are 2 independent parts, one for each index of `parts`. A program takes and returns all parts, laid end to end along the dimension named above; an argument that names none is the same for every part. Nothing has to cross between parts.
Inputs may be any that keep to these rules, and one draw needn't show every extreme that they name: `cache_weight`: entry t equals entry u whenever t == u. `documents`: ids never fall along the tokens; there are 4 prompts of 1 to 32 tokens, one of exactly 32. `page_table`: entries are distinct pool slots; slot q is owned by the device of index q along section+tp (one slot per device). Entries beyond the number of pages are not used.
All inputs are finite; a program needn't handle non-finite values.
Results may differ from a plain program's by a relative error of at most 0.0085.
The roundings to bfloat16 on the way count: a program that leaves them out, or rounds other values in their place, can miss the bound.
Values may be sent and summed in bfloat16 or wider, within the bound.
No kernel may reach another device: no remote copies, remote signals or barrier semaphores. Data moves between devices by JAX's collectives and lax.ppermute only.
A program may use at most 64 MiB of HBM per device.

v0:
```python
import jax
import jax.numpy as jnp
from jax import lax
from jax.sharding import PartitionSpec as P

KV_HEADS = 8
HEAD = 128
PAGE = 8
rope_base = 500000.0


def from_partner(value, axis, distance):
    mask = 2**distance
    pairs = [(source, source ^ mask) for source in range(lax.axis_size(axis))]
    return lax.ppermute(value, axis, pairs)


def document_layout(documents):
    count = documents.shape[0]
    places = jnp.arange(count, dtype=jnp.int32)
    begins = jnp.concatenate([jnp.ones((1,), dtype=bool), documents[1:] != documents[:-1]])
    firsts = lax.cummax(jnp.where(begins, places, jnp.zeros_like(places)), axis=0)
    offsets = places - firsts
    starts = (offsets % PAGE == 0).astype(jnp.int32)
    pages = jnp.cumsum(starts) - 1
    return (offsets, pages)


def rope_tables(offsets, width):
    half_width = width // 2
    freqs = rope_base ** (-(jnp.arange(half_width, dtype=jnp.float32) * 2.0 / width))
    angles = offsets.astype(jnp.float32)[:, None] * freqs[None, :]
    return (jnp.cos(angles), jnp.sin(angles))


def rotate(values, cosines, sines):
    half_width = values.shape[-1] // 2
    first = values[..., :half_width]
    second = values[..., half_width:]
    return jnp.concatenate(
        [first * cosines - second * sines, second * cosines + first * sines], axis=-1
    )


def finish_cache(keyvals, cosines, sines):
    rotated = rotate(keyvals[:, :HEAD], cosines, sines)
    return jnp.concatenate([rotated, keyvals[:, HEAD:]], axis=1).astype(jnp.bfloat16)


def body(prompt_rows, query_weight, cache_weight, output_weight, documents, page_table):
    tp_count = lax.axis_size("tp")
    owners = lax.axis_size(("section", "tp"))
    section = lax.axis_index("section")
    column = lax.axis_index("tp")
    rows_dev = prompt_rows.shape[0]
    half_rows = rows_dev * tp_count
    total_rows = 2 * half_rows
    query_width = query_weight.shape[1]
    query_heads = query_width // HEAD
    replicas = tp_count // KV_HEADS
    slice_width = HEAD // replicas
    head_weight = cache_weight[0]
    offsets, pages = document_layout(documents)
    cosines, sines = rope_tables(offsets, HEAD)
    own_start = section * half_rows
    own_cos = lax.dynamic_slice_in_dim(cosines, own_start, half_rows, 0)
    own_sin = lax.dynamic_slice_in_dim(sines, own_start, half_rows, 0)
    piece = lax.all_gather(prompt_rows, "tp", axis=0, tiled=True)
    query_rows = jnp.dot(piece, query_weight, preferred_element_type=jnp.float32)
    cache_rows = jnp.dot(piece, head_weight, preferred_element_type=jnp.float32)
    joined = jnp.concatenate([query_rows, cache_rows], axis=1)
    query_part = joined[:, :query_width]
    cache_half = finish_cache(joined[:, query_width:], own_cos, own_sin)
    other = from_partner(cache_half, "section", 0)
    lower = jnp.where(section == 0, cache_half, other)
    upper = jnp.where(section == 0, other, cache_half)
    cache_all = jnp.concatenate([lower, upper], axis=0)
    queries = query_part.reshape(half_rows, query_heads, HEAD)
    queries = rotate(queries, own_cos[:, None, :], own_sin[:, None, :]).astype(jnp.bfloat16)
    keys = cache_all[:, :HEAD]
    values = cache_all[:, HEAD:]
    places = jnp.arange(total_rows, dtype=jnp.int32)
    query_places = own_start + jnp.arange(half_rows, dtype=jnp.int32)
    query_docs = lax.dynamic_slice_in_dim(documents, own_start, half_rows, 0)
    allowed = (query_docs[:, None] == documents[None, :]) & (
        places[None, :] <= query_places[:, None]
    )
    scale = 1.0 / HEAD**0.5
    scores = jnp.einsum("qhd,kd->hqk", queries, keys, preferred_element_type=jnp.float32) * scale
    scores = jnp.where(allowed[None, :, :], scores, -jnp.inf)
    weights = jax.nn.softmax(scores, axis=-1).astype(jnp.bfloat16)
    mixed = jnp.einsum("hqk,kd->qhd", weights, values, preferred_element_type=jnp.float32)
    attention = mixed.astype(jnp.bfloat16).reshape(half_rows, query_heads * HEAD)
    summed = lax.psum_scatter(
        jnp.dot(attention, output_weight, preferred_element_type=jnp.float32),
        "tp",
        scatter_dimension=0,
        tiled=True,
    )
    branch_output = summed.astype(jnp.bfloat16)
    column_start = section * HEAD + column % replicas * slice_width
    share = lax.dynamic_slice_in_dim(cache_all, column_start, slice_width, 1)
    capacity = rows_dev // 4 * PAGE
    row_of = page_table[pages] * PAGE + offsets % PAGE
    outgoing = jnp.zeros((owners * capacity, slice_width), jnp.bfloat16).at[row_of].set(share)
    outgoing = outgoing.reshape(owners, capacity, slice_width)
    arrived = lax.all_to_all(outgoing, ("section", "tp"), split_axis=0, concat_axis=2, tiled=True)
    return (branch_output, arrived)


def solution(mesh):
    return jax.shard_map(
        body,
        mesh=mesh,
        in_specs=(
            P(("parts", "section", "tp"), None),
            P(None, "tp"),
            P("tp", None, None),
            P("tp", None),
            P("parts"),
            P("parts"),
        ),
        out_specs=(P(("parts", "section", "tp"), None), P(("parts", "section", "tp"), None, None)),
        check_vma=False,
    )
```

profile of v0, /device:TPU:0, one launch (start us, length us, event | category | flops | bytes accessed | tf_op | source)
XLA Modules:
  0.0 150.3 jit_solution(4755525236660970167)
XLA Ops:
  0.6 0.0 copy-start.1
  0.6 0.0 copy-start
  0.7 1.8 %fusion.44 = (s32[1]{0:T(128)}, s32[1]{0:T(128)}, s32[1]{0:T(128)}, s32[1]{0:T(128)}, s32[1]{0:T(128)}, /*index=5*/s32[1]{0:T(128)}, s32[1]{0:T(128)}, s32[1]{0:...) fusion(s32[12]{0:T(128)} %param.11), kind=kLoop, calls=%fused_computation.74 | loop fusion | bytes 96 | tf_op jit(solution)/shard_map/gather | solution.py:104
  2.5 0.8 compare_bitcast_fusion
  3.3 0.1 add_select_fusion.1
  3.3 0.1 copy.18
  3.4 0.1 reduce-window.6
  3.6 0.1 reduce-window.9
  3.7 0.2 compare_reduce_fusion.4
  3.9 4.4 %select_reduce_fusion = s32[64]{0:T(128)S(1)} fusion(s32[]{:T(128)} %bitcast.12, s32[]{:T(128)} %bitcast.13, s32[]{:T(128)} %bitcast.14, s32[]{:T(128)} %bitcast.15, s32[]{:T(128)} %bitcast.16, s32[]{:T(128)} %bitcast.18, s32[]{:T(128)} %bitcast.17, s32[64,1]{1,0:T(8,128)S(1)} %reduce-window.9), kind=kLoop, calls=%fused_computation.35 | loop fusion | flops 1024 | bytes 540 | tf_op jit(solution)/shard_map/gather | solution.py:104
  8.3 3.2 %fusion.31 = s32[64,1]{0,1:T(1,128)S(1)} fusion(pred[64]{0:T(512)(128)(4,1)S(1)} %get-tuple-element.8, pred[64]{0:T(512)(128)(4,1)S(1)} %get-tuple-element.5, pred[64]{0:T(512)(128)(4,1)S(1)} %get-tuple-element.6, pred[64]{0:T(512)(128)(4,1)S(1)} %get-tuple-element.7, pred[64]{0:T(512)(128)(4,1)S(1)} %get-tuple-element.4, s32[64]{0:T(128)S(1)} %select_reduce_fusion, ...), kind=kLoop, calls=%fused_computation.63 | loop fusion | flops 384 | bytes 852 | tf_op jit(solution)/shard_map/mul | solution.py:104
  11.5 0.1 copy.22
  11.6 0.1 fusion.15
  11.7 33.3 %all-gather = bf16[8,4,8192]{2,1,0:T(4,128)(2,1)S(1)} all-gather(bf16[1,4,8192]{2,1,0:T(4,128)(2,1)} %bitcast.64), channel_id=1, replica_groups=mesh['parts'=2,'section'=2,'tp'=8] {'tp'}, dimensions={0}, use_global_device_ids=true | all-gather | bytes 589824 | tf_op jit(solution)/shard_map/all_gather | solution.py:68
  45.0 0.1 reshape.264
  45.1 3.0 %fusion.1 = f32[32,256]{1,0:T(8,128)S(1)} fusion(bf16[32,8192]{1,0:T(8,128)(2,1)S(1)} %reshape.264, bf16[1,8192,256]{2,1,0:T(8,128)(2,1)} %param.8), kind=kOutput, calls=%fused_computation.2 | convolution fusion | flops 134217728 | bytes 4751360 | tf_op jit(solution)/shard_map/dot_general | solution.py:70
  48.2 0.1 broadcast_multiply_fusion
  48.2 0.1 subtract_convert_fusion.1
  48.3 0.1 add_convert_fusion.1
  48.4 0.1 pad_maximum_fusion
  48.5 0.0 collective-permute-start
  48.5 0.7 dynamic_slice.14
  49.2 8.7 %convolution_bitcast_fusion = f32[4,8,8,128]{3,1,2,0:T(8,128)S(1)} fusion(bf16[32,8192]{1,0:T(8,128)(2,1)S(1)} %reshape.264, bf16[8192,1024]{1,0:T(8,128)(2,1)} %param.7), kind=kOutput, calls=%fused_computation.6 | convolution fusion | flops 536870912 | bytes 17432576 | tf_op jit(solution)/shard_map/dot_general | solution.py:69
  58.0 0.1 fusion.43
  58.1 0.1 subtract_convert_fusion
  58.2 0.0 copy-done
  58.2 0.1 fusion.26
  58.3 0.0 copy-done.1
  58.3 0.6 dynamic-slice
  59.5 0.0 collective-permute-done
  59.5 0.1 broadcast_select_fusion
  59.6 1.3 scatter_custom_fusion
  60.9 5.8 %all-to-all-start = ((bf16[16,8,128]{2,1,0:T(8,128)(2,1)}), bf16[16,8,128]{2,1,0:T(8,128)(2,1)S(1)}, u32[]{:S(2)}, u32[]{:S(2)}) async-start(bf16[16,8,128]{2,1,0:T(8,128)(2,1)} %bitcast.20), calls=%async_computation | async-start | bytes 65536 | tf_op jit(solution)/shard_map/all_to_all | solution.py:107
  66.7 0.4 fusion.45
  67.2 0.2 fusion.7
  67.4 8.7 %fusion.8 = f32[32,8192]{1,0:T(8,128)S(1)} fusion(bf16[1024,8192]{1,0:T(8,128)(2,1)} %param.9, bf16[8,4,8,128]{3,2,1,0:T(8,128)(2,1)S(1)} %fusion.7), kind=kOutput, calls=%fused_computation.18 | convolution fusion | flops 536870912 | bytes 17891328 | tf_op jit(solution)/shard_map/dot_general | solution.py:95
  76.1 72.9 %all-reduce.2 = bf16[32,8192]{1,0:T(8,128)(2,1)S(1)} all-reduce(f32[32,8192]{1,0:T(8,128)S(1)} %fusion.8), channel_id=2, replica_groups=mesh['parts'=2,'section'=2,'tp'=8] {'tp'}, use_global_device_ids=true, to_apply=%region_3.4.clone | all-reduce | flops 262144 | bytes 1572864
  149.0 0.7 dynamic-slice_convert_fusion
  149.7 0.0 all-to-all-done
  149.7 0.6 copy.45
  (6 shorter events, 0.1 us)
Async XLA Ops:
  0.6 57.6 %copy-start.1 = (u32[32]{0:T(128)S(1)}, u32[32]{0:T(128)}, u32[]{:S(2)}) copy-start(u32[32]{0:T(128)} %constant.96) | copy-start | bytes 388
  0.6 57.5 %copy-start = (s32[64]{0:T(128)S(1)}, s32[64]{0:T(128)}, u32[]{:S(2)}) copy-start(s32[64]{0:T(128)} %param.10) | copy-start | bytes 772
  48.5 11.0 %collective-permute-start = (bf16[32,256]{1,0:T(8,128)(2,1)S(1)}, bf16[32,256]{1,0:T(8,128)(2,1)S(1)}, u32[]{:S(2)}, u32[]{:S(2)}) collective-permute-start(bf16[32,256]{1,0:T(8,128)(2,1)S(1)} %pad_maximum_fusion), channel_id=1, source_target_pairs={{0,8},{8,0},{1,9},{9,1},{2,10},{10,2},{3,11},{11,3},{4,12},{12,4},... | collective-permute-start | bytes 49160 | tf_op jit(solution)/shard_map/ppermute | solution.py:15
  60.9 88.8 %all-to-all-start = ((bf16[16,8,128]{2,1,0:T(8,128)(2,1)}), bf16[16,8,128]{2,1,0:T(8,128)(2,1)S(1)}, u32[]{:S(2)}, u32[]{:S(2)}) async-start(bf16[16,8,128]{2,1,0:T(8,128)(2,1)} %bitcast.20), calls=%async_computation | async-start | bytes 65536 | tf_op jit(solution)/shard_map/all_to_all | solution.py:107
where the time goes:
time: 151 us; the launch traced here: 150 us
  blocking collectives  106 us (70%)
  matrix products  21.1 us (14%)
  other arithmetic  10.9 us (7%)
  starting transfers between devices  5.83 us (4%)
  local copies, waits for them, and re-layouts  4.85 us (3%)
    unnamed x1, blocking collectives  72.9 us
    all_gather x1, blocking collectives, body(): piece = lax.all_gather(prompt_rows, 'tp', axis=0, tiled=True)  33.3 us
    dot_general x1, matrix products, body(): jnp.dot(attention, output_weight, preferred_element_type=jnp.float32)  8.75 us
    dot_general x1, matrix products, body(): jnp.dot(piece, query_weight, preferred_element_type=jnp.float32)  8.75 us
    all_to_all x1, starting transfers between devices, body(): lax.all_to_all(outgoing, ('section', 'tp'), split_axis=0, concat_axis=2,...  5.82 us
    gather x2, other arithmetic, body(): row_of = page_table[pages] * PAGE + offsets % PAGE  4.6 us
    mul x1, other arithmetic, body(): row_of = page_table[pages] * PAGE + offsets % PAGE  3.23 us
  transfers between devices with their start and end apart: 2, of which 0 were waited for; matrix products, arithmetic and copies ran while one was open for 14% of the time, Pallas kernels for 0%

commit v1 on v0

--- a/solution.py
+++ b/solution.py
@@ -7,6 +7,21 @@
 HEAD = 128
 PAGE = 8
 rope_base = 500000.0
+
+
+def spread_trails_all(message):
+    t_next, known = (lax.axis_size("tp"), lax.axis_index("tp"))
+    local_part, item_now = (message, 1)
+    while item_now < t_next:
+        slots = []
+        for d in range(t_next):
+            slots.append((d, d ^ item_now))
+        row_out = lax.ppermute(local_part, axis_name="tp", perm=slots)
+        tile_out = jnp.concatenate([local_part, row_out], axis=0)
+        val = jnp.concatenate([row_out, local_part], axis=0)
+        local_part = jnp.where(known & item_now == 0, tile_out, val)
+        item_now = 2 * item_now
+    return local_part
 
 
 def from_partner(value, axis, distance):
@@ -65,7 +80,7 @@
     own_start = section * half_rows
     own_cos = lax.dynamic_slice_in_dim(cosines, own_start, half_rows, 0)
     own_sin = lax.dynamic_slice_in_dim(sines, own_start, half_rows, 0)
-    piece = lax.all_gather(prompt_rows, "tp", axis=0, tiled=True)
+    piece = spread_trails_all(prompt_rows)
     query_rows = jnp.dot(piece, query_weight, preferred_element_type=jnp.float32)
     cache_rows = jnp.dot(piece, head_weight, preferred_element_type=jnp.float32)
     joined = jnp.concatenate([query_rows, cache_rows], axis=1)

time: 151 us -> 138 us (0.914)
  blocking collectives: 106 us -> 72.9 us
  waiting for transfers between devices: 0.01 us -> 12 us
  starting transfers between devices: 5.83 us -> 12.3 us
  other arithmetic: 10.9 us -> 12.7 us
    all_gather x1 -> x0, blocking collectives: 33.3 us -> none  [body(): piece = lax.all_gather(prompt_rows, 'tp', axis=0, tiled=True)]
    ppermute x0 -> x3, waiting for transfers between devices: none -> 12 us  [spread_trails_all(): row_out = lax.ppermute(local_part, axis_name='tp', perm=slots)]
    ppermute x0 -> x3, starting transfers between devices: none -> 7.33 us  [spread_trails_all(): row_out = lax.ppermute(local_part, axis_name='tp', perm=slots)]
  transfers between devices with their start and end apart: 2 -> 5, of which waited for: 0 -> 2; matrix products, arithmetic and copies ran while one was open for 14% -> 24% of each run, Pallas kernels for 0% -> 0%
where the time goes in v1:
time: 138 us
  blocking collectives  72.9 us (53%)
  matrix products  21.1 us (15%)
  other arithmetic  12.7 us (9%)
  starting transfers between devices  12.3 us (9%)
  waiting for transfers between devices  12 us (9%)
  local copies, waits for them, and re-layouts  5.36 us (4%)
  between operations  1.42 us (1%)
    unnamed x1, blocking collectives  72.9 us
    ppermute x3, waiting for transfers between devices, spread_trails_all(): row_out = lax.ppermute(local_part, axis_name='tp', perm=slots)  12 us
    dot_general x1, matrix products, body(): jnp.dot(attention, output_weight, preferred_element_type=jnp.float32)  8.75 us
    dot_general x1, matrix products, body(): jnp.dot(piece, query_weight, preferred_element_type=jnp.float32)  8.75 us
    ppermute x3, starting transfers between devices, spread_trails_all(): row_out = lax.ppermute(local_part, axis_name='tp', perm=slots)  7.33 us
    all_to_all x1, starting transfers between devices, body(): lax.all_to_all(outgoing, ('section', 'tp'), split_axis=0, concat_axis=2,...  4.97 us
    gather x2, other arithmetic, body(): row_of = page_table[pages] * PAGE + offsets % PAGE  4.6 us
    mul x1, other arithmetic, body(): row_of = page_table[pages] * PAGE + offsets % PAGE  3.23 us
  transfers between devices with their start and end apart: 5, of which 2 were waited for; matrix products, arithmetic and copies ran while one was open for 24% of the time, Pallas kernels for 0%

profile of v1, /device:TPU:0, one launch (start us, length us, event | category | flops | bytes accessed | tf_op | source)
XLA Modules:
  0.0 137.7 jit_solution(6664151013857171222)
XLA Ops:
  0.6 3.0 %collective-permute-start = (bf16[4,8192]{1,0:T(4,128)(2,1)}, bf16[4,8192]{1,0:T(4,128)(2,1)S(1)}, u32[]{:S(2)}, u32[]{:S(2)}) collective-permute-start(bf16[4,8192]{1,0:T(4,128)(2,1)} %param.6), channel_id=1, source_target_pairs={{0,1},{1,0},{2,3},{3,2},{4,5},{5,4},{6,7},{7,6},{8,9},{9,8},{10,11... | collective-permute-start | bytes 196616 | tf_op jit(solution)/shard_map/ppermute | solution.py:19
  3.7 1.8 %fusion.46 = (s32[1]{0:T(128)}, s32[1]{0:T(128)}, s32[1]{0:T(128)}, s32[1]{0:T(128)}, s32[1]{0:T(128)}, /*index=5*/s32[1]{0:T(128)}, s32[1]{0:T(128)}, s32[1]{0:...) fusion(s32[12]{0:T(128)} %param.11), kind=kLoop, calls=%fused_computation.79 | loop fusion | bytes 96 | tf_op jit(solution)/shard_map/gather | solution.py:119
  5.4 0.8 compare_bitcast_fusion
  6.3 0.1 add_select_fusion.1
  6.3 0.1 copy.18
  6.4 0.1 reduce-window.6
  6.6 0.1 reduce-window.9
  6.7 0.2 compare_reduce_fusion.4
  6.9 4.4 %select_reduce_fusion = s32[64]{0:T(128)S(1)} fusion(s32[]{:T(128)} %bitcast.11, s32[]{:T(128)} %bitcast.12, s32[]{:T(128)} %bitcast.13, s32[]{:T(128)} %bitcast.14, s32[]{:T(128)} %bitcast.15, s32[]{:T(128)} %bitcast.17, s32[]{:T(128)} %bitcast.16, s32[64,1]{1,0:T(8,128)S(1)} %reduce-window.9), kind=kLoop, calls=%fused_computation.38 | loop fusion | flops 1024 | bytes 540 | tf_op jit(solution)/shard_map/gather | solution.py:119
  11.3 3.2 %fusion.31 = s32[64,1]{0,1:T(1,128)S(1)} fusion(pred[64]{0:T(512)(128)(4,1)S(1)} %get-tuple-element.8, pred[64]{0:T(512)(128)(4,1)S(1)} %get-tuple-element.5, pred[64]{0:T(512)(128)(4,1)S(1)} %get-tuple-element.6, pred[64]{0:T(512)(128)(4,1)S(1)} %get-tuple-element.7, pred[64]{0:T(512)(128)(4,1)S(1)} %get-tuple-element.4, s32[64]{0:T(128)S(1)} %select_reduce_fusion, ...), kind=kLoop, calls=%fused_computation.66 | loop fusion | flops 384 | bytes 852 | tf_op jit(solution)/shard_map/mul | solution.py:119
  14.5 0.1 copy.22
  14.6 0.7 dynamic_slice.14
  15.3 0.7 fusion.26
  16.1 0.1 fusion.15
  16.2 0.0 collective-permute-done
  16.2 1.0 maximum_select_fusion.2
  17.3 1.6 %collective-permute-start.1 = (bf16[8,8192]{1,0:T(8,128)(2,1)S(1)}, bf16[8,8192]{1,0:T(8,128)(2,1)S(1)}, u32[]{:S(2)}, u32[]{:S(2)}) collective-permute-start(bf16[8,8192]{1,0:T(8,128)(2,1)S(1)} %maximum_select_fusion.2), channel_id=1, source_target_pairs={{0,2},{1,3},{2,0},{3,1},{4,6},{5,7},{6,4},{7,5},{8,10},{9,11},{10,... | collective-permute-start | bytes 393224 | tf_op jit(solution)/shard_map/ppermute | solution.py:19
  18.9 3.4 %collective-permute-done.1 = bf16[8,8192]{1,0:T(8,128)(2,1)S(1)} collective-permute-done((bf16[8,8192]{1,0:T(8,128)(2,1)S(1)}, bf16[8,8192]{1,0:T(8,128)(2,1)S(1)}, u32[]{:S(2)}, u32[]{:S(2)}) %collective-permute-start.1) | collective-permute-done | bytes 131104 | tf_op jit(solution)/shard_map/ppermute | solution.py:19
  22.3 2.7 %collective-permute-start.2 = (bf16[16,8192]{1,0:T(8,128)(2,1)S(1)}, bf16[16,8192]{1,0:T(8,128)(2,1)S(1)}, u32[]{:S(2)}, u32[]{:S(2)}) collective-permute-start(bf16[16,8192]{1,0:T(8,128)(2,1)S(1)} %maximum_select_fusion.1), channel_id=1, source_target_pairs={{0,4},{1,5},{2,6},{3,7},{4,0},{5,1},{6,2},{7,3},{8,12},{9,13},{10,... | collective-permute-start | bytes 786440 | tf_op jit(solution)/shard_map/ppermute | solution.py:19
  25.0 1.2 dynamic-slice
  26.9 0.1 broadcast_multiply_fusion
  27.0 8.6 %collective-permute-done.2 = bf16[16,8192]{1,0:T(8,128)(2,1)S(1)} collective-permute-done((bf16[16,8192]{1,0:T(8,128)(2,1)S(1)}, bf16[16,8192]{1,0:T(8,128)(2,1)S(1)}, u32[]{:S(2)}, u32[]{:S(2)}) %collective-permute-start.2) | collective-permute-done | bytes 262176 | tf_op jit(solution)/shard_map/ppermute | solution.py:19
  35.5 3.0 %fusion.1 = f32[32,256]{1,0:T(8,128)S(1)} fusion(bf16[1,8192,256]{2,1,0:T(8,128)(2,1)} %param.8, bf16[16,8192]{1,0:T(8,128)(2,1)S(1)} %collective-permute-done.2, bf16[16,8192]{1,0:T(8,128)(2,1)S(1)} %maximum_select_fusion.1, pred[]{:T(512)S(6)} %eq.46), kind=kOutput, calls=%fused_computation.2 | convolution fusion | flops 136577024 | bytes 4751361 | tf_op jit(solution)/shard_map/dot_general | solution.py:85
  38.6 0.1 subtract_convert_fusion.1
  38.6 0.1 add_convert_fusion.1
  38.7 0.1 pad_maximum_fusion
  38.8 0.0 collective-permute-start.3
  38.8 8.7 %convolution_bitcast_fusion = f32[4,8,8,128]{3,1,2,0:T(8,128)S(1)} fusion(bf16[8192,1024]{1,0:T(8,128)(2,1)} %param.7, bf16[16,8192]{1,0:T(8,128)(2,1)S(1)} %collective-permute-done.2, bf16[16,8192]{1,0:T(8,128)(2,1)S(1)} %maximum_select_fusion.1, pred[]{:T(512)S(6)} %eq.46), kind=kOutput, calls=%fused_computation.6 | convolution fusion | flops 539230208 | bytes 17432576 | tf_op jit(solution)/shard_map/dot_general | solution.py:84
  47.6 0.1 fusion.45
  47.7 0.1 subtract_convert_fusion
  47.8 0.0 collective-permute-done.3
  47.8 0.1 broadcast_select_fusion
  47.9 1.3 scatter_custom_fusion
  49.2 5.0 %all-to-all-start = ((bf16[16,8,128]{2,1,0:T(8,128)(2,1)}), bf16[16,8,128]{2,1,0:T(8,128)(2,1)S(1)}, u32[]{:S(2)}, u32[]{:S(2)}) async-start(bf16[16,8,128]{2,1,0:T(8,128)(2,1)} %bitcast.19), calls=%async_computation | async-start | bytes 65536 | tf_op jit(solution)/shard_map/all_to_all | solution.py:122
  54.2 0.4 fusion.47
  54.6 0.2 fusion.7
  54.8 8.7 %fusion.8 = f32[32,8192]{1,0:T(8,128)S(1)} fusion(bf16[1024,8192]{1,0:T(8,128)(2,1)} %param.9, bf16[8,4,8,128]{3,2,1,0:T(8,128)(2,1)S(1)} %fusion.7), kind=kOutput, calls=%fused_computation.21 | convolution fusion | flops 536870912 | bytes 17891328 | tf_op jit(solution)/shard_map/dot_general | solution.py:110
  63.5 72.9 %all-reduce.2 = bf16[32,8192]{1,0:T(8,128)(2,1)S(1)} all-reduce(f32[32,8192]{1,0:T(8,128)S(1)} %fusion.8), channel_id=2, replica_groups=mesh['parts'=2,'section'=2,'tp'=8] {'tp'}, use_global_device_ids=true, to_apply=%region_3.4.clone | all-reduce | flops 262144 | bytes 1572864
  136.4 0.7 dynamic-slice_convert_fusion
  137.1 0.0 all-to-all-done
  137.1 0.6 copy.48
  (7 shorter events, 0.1 us)
Async XLA Ops:
  0.6 15.6 %collective-permute-start = (bf16[4,8192]{1,0:T(4,128)(2,1)}, bf16[4,8192]{1,0:T(4,128)(2,1)S(1)}, u32[]{:S(2)}, u32[]{:S(2)}) collective-permute-start(bf16[4,8192]{1,0:T(4,128)(2,1)} %param.6), channel_id=1, source_target_pairs={{0,1},{1,0},{2,3},{3,2},{4,5},{5,4},{6,7},{7,6},{8,9},{9,8},{10,11... | collective-permute-start | bytes 196616 | tf_op jit(solution)/shard_map/ppermute | solution.py:19
  17.3 5.0 %collective-permute-start.1 = (bf16[8,8192]{1,0:T(8,128)(2,1)S(1)}, bf16[8,8192]{1,0:T(8,128)(2,1)S(1)}, u32[]{:S(2)}, u32[]{:S(2)}) collective-permute-start(bf16[8,8192]{1,0:T(8,128)(2,1)S(1)} %maximum_select_fusion.2), channel_id=1, source_target_pairs={{0,2},{1,3},{2,0},{3,1},{4,6},{5,7},{6,4},{7,5},{8,10},{9,11},{10,... | collective-permute-start | bytes 393224 | tf_op jit(solution)/shard_map/ppermute | solution.py:19
  22.3 13.2 %collective-permute-start.2 = (bf16[16,8192]{1,0:T(8,128)(2,1)S(1)}, bf16[16,8192]{1,0:T(8,128)(2,1)S(1)}, u32[]{:S(2)}, u32[]{:S(2)}) collective-permute-start(bf16[16,8192]{1,0:T(8,128)(2,1)S(1)} %maximum_select_fusion.1), channel_id=1, source_target_pairs={{0,4},{1,5},{2,6},{3,7},{4,0},{5,1},{6,2},{7,3},{8,12},{9,13},{10,... | collective-permute-start | bytes 786440 | tf_op jit(solution)/shard_map/ppermute | solution.py:19
  38.8 9.0 %collective-permute-start.3 = (bf16[32,256]{1,0:T(8,128)(2,1)S(1)}, bf16[32,256]{1,0:T(8,128)(2,1)S(1)}, u32[]{:S(2)}, u32[]{:S(2)}) collective-permute-start(bf16[32,256]{1,0:T(8,128)(2,1)S(1)} %pad_maximum_fusion), channel_id=1, source_target_pairs={{0,8},{8,0},{1,9},{9,1},{2,10},{10,2},{3,11},{11,3},{4,12},{12,4},... | collective-permute-start | bytes 49160 | tf_op jit(solution)/shard_map/ppermute | solution.py:30
  49.2 87.9 %all-to-all-start = ((bf16[16,8,128]{2,1,0:T(8,128)(2,1)}), bf16[16,8,128]{2,1,0:T(8,128)(2,1)S(1)}, u32[]{:S(2)}, u32[]{:S(2)}) async-start(bf16[16,8,128]{2,1,0:T(8,128)(2,1)} %bitcast.19), calls=%async_computation | async-start | bytes 65536 | tf_op jit(solution)/shard_map/all_to_all | solution.py:122
